TPU v7x, 32 devices: a whole 2x2x4 slice. The times are simulated.
32 devices in a mesh: clip: 2 (over y), seq: 4 (over z), head: 4 (over x, core).
Axes of the slice: x: 2, y: 2, z: 4, core: 2. Of those that a mesh axis runs over, the one named last changes fastest.
Arguments:
- queries: bfloat16 [16, 4, 16, 3072], P(('clip', 'head'), 'seq'), parts along dimension 0, may hold values from -15 to 15
- attn_keys: bfloat16 [16, 4, 16, 3072], P(('clip', 'head'), 'seq'), parts along dimension 0, may hold values from -5 to 5
- attn_values: bfloat16 [16, 4, 16, 3072], P(('clip', 'head'), 'seq'), parts along dimension 0, may hold values from -5 to 5
- residual: bfloat16 [16, 4, 16, 5120], P(('clip', 'head'), 'seq'), parts along dimension 0, may hold values from -6 to 6
- out_weight: bfloat16 [3072, 5120], P('head', 'seq'), may hold values from -0.109375 to 0.109375
- out_gate: float32 [5120], replicated, may hold values from 0.3 to 3
- head_shift: float32 [5120], replicated, may hold values from -3 to 3
- head_scale: float32 [5120], replicated, may hold values from -1.5 to 1.5
- head_weight: bfloat16 [5120, 64], replicated, may hold values from -0.078125 to 0.078125
- head_bias: float32 [64], replicated, may hold values from -3 to 3
- conv_weight: bfloat16 [3, 3, 3, 16, 384], replicated, may hold values from -0.3125 to 0.3125
- conv_bias: float32 [384], replicated, may hold values from -3 to 3
- norm_gain: float32 [384], replicated, may hold values from 0.5 to 2
Outputs:
- hidden: bfloat16 [16, 4, 16, 5120], P(('clip', 'head'), 'seq'), parts along dimension 0
- features: bfloat16 [16, 8, 32, 384], P(('clip', 'head'), 'seq'), parts along dimension 0
There are 2 independent parts, one for each index of `clip`. A program takes and returns all parts, laid end to end along the dimension named above; an argument that names none is the same for every part. Nothing has to cross between parts.
All inputs are finite; a program needn't handle non-finite values.
Results may differ from a plain program's by a relative error of at most 0.013.
Values may be sent and summed in bfloat16 or wider, within the bound.
No kernel may reach another device: no remote copies, remote signals or barrier semaphores. Data moves between devices by JAX's collectives and lax.ppermute only.
A program may use at most 128 MiB of HBM per device.

v0:
```python
import jax
import jax.numpy as jnp
from jax import lax
from jax.sharding import PartitionSpec as P

HEAD_DIM = 128


def from_behind(value, axis, steps):
    count = lax.axis_size(axis)
    first, last = (max(0, -steps), min(count, count - steps))
    return lax.ppermute(value, axis, [(source, source + steps) for source in range(first, last)])


def padded_2(x, sides, width):
    for axis, dim in sides:
        peers, length = (lax.axis_size(axis), x.shape[dim])
        up = [(i, (i + 1) % peers) for i in range(peers - 1)]
        down = [(j, i) for i, j in up]
        last = lax.slice_in_dim(x, length - width, length, axis=dim)
        first = lax.slice_in_dim(x, 0, width, axis=dim)
        before = lax.ppermute(last, axis, up)
        after = lax.ppermute(first, axis, down)
        x = jnp.concatenate([before, x, after], axis=dim)
    return x


def head_latent(hidden, head_shift, head_scale, head_weight, head_bias):
    values = hidden.astype(jnp.float32)
    center = values - jnp.mean(values, -1, keepdims=True)
    spread = jnp.mean(center * center, -1, keepdims=True)
    normed = (center * lax.rsqrt(spread + 1e-06) * (1.0 + head_scale) + head_shift).astype(
        jnp.bfloat16
    )
    flat = normed.reshape(-1, normed.shape[-1])
    latent = (jnp.dot(flat, head_weight, preferred_element_type=jnp.float32) + head_bias).astype(
        jnp.bfloat16
    )
    frames, height, breadth = (hidden.shape[0], hidden.shape[1], hidden.shape[2])
    channels = head_weight.shape[1] // 4
    patches = latent.reshape(frames, height, breadth, 2, 2, channels).transpose(0, 1, 3, 2, 4, 5)
    return patches.reshape(frames, height * 2, breadth * 2, channels)


def convolve(padded, frames, conv_weight, conv_bias, norm_gain):
    height = padded.shape[1] - 2
    breadth = padded.shape[2] - 2
    stacked = jnp.concatenate(
        [
            padded[
                time_off : time_off + frames,
                row_off : row_off + height,
                col_off : col_off + breadth,
            ]
            for time_off in range(3)
            for row_off in range(3)
            for col_off in range(3)
        ],
        -1,
    )
    kernel = conv_weight.reshape(-1, conv_weight.shape[-1])
    linear = (
        jnp.dot(stacked.reshape(-1, stacked.shape[-1]), kernel, preferred_element_type=jnp.float32)
        + conv_bias
    )
    normed = linear * lax.rsqrt(jnp.mean(linear * linear, -1, keepdims=True) + 1e-06) * norm_gain
    return jax.nn.silu(normed).astype(jnp.bfloat16).reshape(frames, height, breadth, -1)


def attend_block(carried, block_keys, block_values, query_heads):
    running, denominator, weighted = carried
    scores = jnp.einsum("hqd,khd->hqk", query_heads, block_keys, preferred_element_type=jnp.float32)
    scores = scores * query_heads.shape[-1] ** (-0.5)
    newmax = jnp.maximum(running, jnp.max(scores, -1))
    factor = jnp.exp(running - newmax)
    weights = jnp.exp(scores - newmax[..., None])
    denominator = denominator * factor + jnp.sum(weights, -1)
    product = jnp.einsum(
        "hqk,khd->hqd",
        weights.astype(jnp.bfloat16),
        block_values,
        preferred_element_type=jnp.float32,
    )
    weighted = weighted * factor[..., None] + product
    return (newmax, denominator, weighted)


def fold_pieces(query_heads, carried, pieces):
    key_piece, value_piece = pieces
    frames, height, breadth = (key_piece.shape[0], key_piece.shape[1], key_piece.shape[2])
    heads_here, head_width = (query_heads.shape[0], query_heads.shape[2])
    group_rows = 4

    def regroup(one_piece):
        shaped = one_piece.reshape(
            frames, height // group_rows, group_rows, breadth, heads_here, head_width
        )
        shaped = shaped.transpose(1, 0, 2, 3, 4, 5)
        return shaped.reshape(
            height // group_rows, frames * group_rows * breadth, heads_here, head_width
        )

    def advance(inner, blocks):
        return (attend_block(inner, blocks[0], blocks[1], query_heads), None)

    carried, _ = lax.scan(advance, carried, (regroup(key_piece), regroup(value_piece)))
    return carried


def on_device(
    queries,
    attn_keys,
    attn_values,
    residual,
    out_weight,
    out_gate,
    head_shift,
    head_scale,
    head_weight,
    head_bias,
    conv_weight,
    conv_bias,
    norm_gain,
):
    head_count = lax.axis_size("head")
    frames_dev = queries.shape[0]
    group_width = queries.shape[3] // head_count
    head_width = HEAD_DIM
    heads_here = group_width // head_width
    local_queries, local_keys, local_values = (
        lax.all_to_all(queries, "head", split_axis=3, concat_axis=0, tiled=True),
        lax.all_to_all(attn_keys, "head", split_axis=3, concat_axis=0, tiled=True),
        lax.all_to_all(attn_values, "head", split_axis=3, concat_axis=0, tiled=True),
    )
    frames_all, height, breadth = (
        local_queries.shape[0],
        local_queries.shape[1],
        local_queries.shape[2],
    )
    count = frames_all * height * breadth
    query_heads = local_queries.reshape(count, heads_here, head_width).transpose(1, 0, 2)
    initial = (
        jnp.full((heads_here, count), -1e30, jnp.float32),
        jnp.zeros((heads_here, count), jnp.float32),
        jnp.zeros((heads_here, count, head_width), jnp.float32),
    )
    carried = fold_pieces(
        query_heads,
        initial,
        (
            lax.all_gather(local_keys, "seq", axis=1, tiled=True),
            lax.all_gather(local_values, "seq", axis=1, tiled=True),
        ),
    )
    running, denominator, weighted = carried
    attended = (weighted / denominator[..., None]).astype(jnp.bfloat16)
    attended = attended.transpose(1, 0, 2).reshape(count, group_width)
    partial_value = jnp.dot(
        attended,
        lax.all_gather(out_weight, "seq", axis=1, tiled=True),
        preferred_element_type=jnp.float32,
    )
    partial_value = partial_value.reshape(frames_all, height, breadth, partial_value.shape[-1])
    owned = lax.psum_scatter(
        partial_value.astype(jnp.bfloat16), "head", scatter_dimension=0, tiled=True
    ).astype(jnp.float32)
    hidden = (residual.astype(jnp.float32) + out_gate * owned).astype(jnp.bfloat16)
    own_video = head_latent(hidden, head_shift, head_scale, head_weight, head_bias)
    earlier = from_behind(own_video, "head", 1)
    video = jnp.concatenate([earlier, own_video], 0)
    extended = padded_2(video, (("seq", 1),), 1)
    padded = jnp.pad(extended, ((0, 0), (0, 0), (1, 1), (0, 0)))
    features = convolve(padded, frames_dev, conv_weight, conv_bias, norm_gain)
    return (hidden, features)


def solution(mesh):
    return jax.shard_map(
        on_device,
        mesh=mesh,
        in_specs=(
            P(("clip", "head"), "seq", None, None),
            P(("clip", "head"), "seq", None, None),
            P(("clip", "head"), "seq", None, None),
            P(("clip", "head"), "seq", None, None),
            P("head", "seq"),
            P(),
            P(),
            P(),
            P(),
            P(),
            P(),
            P(),
            P(),
        ),
        out_specs=(P(("clip", "head"), "seq", None, None), P(("clip", "head"), "seq", None, None)),
        check_vma=False,
    )
```

profile of v0, /device:TPU:2, one launch (start us, length us, event | category | flops | bytes accessed | tf_op | source)
XLA Modules:
  0.0 232.1 jit_solution(3632974338613475676)
XLA Ops:
  7.2 0.0 copy-start
  7.2 0.0 all-gather.2.cloned.1.call-start
  7.2 0.7 all-gather.2.cloned.1.call-update
  7.9 0.2 copy-done.5
  8.2 1.8 copy.79
  10.0 2.3 reshape.122
  12.3 3.4 %all-to-all-start.1 = ((bf16[4,2,12288]{2,1,0:T(2,128)(2,1)}), bf16[4,2,12288]{2,1,0:T(2,128)(2,1)S(1)}, u32[]{:S(2)}, u32[]{:S(2)}) async-start(bf16[4,2,12288]{2,1,0:T(2,128)(2,1)} %reshape.122), calls=%async_computation.1 | async-start | bytes 393216 | tf_op jit(solution)/shard_map/all_to_all | solution.py:132
  15.6 1.8 copy.75
  17.5 0.0 copy-start.7
  17.5 2.3 reshape.124
  19.8 4.4 %all-to-all-start = ((bf16[4,2,12288]{2,1,0:T(2,128)(2,1)}), bf16[4,2,12288]{2,1,0:T(2,128)(2,1)S(1)}, u32[]{:S(2)}, u32[]{:S(2)}) async-start(bf16[4,2,12288]{2,1,0:T(2,128)(2,1)} %reshape.124), calls=%async_computation | async-start | bytes 393216 | tf_op jit(solution)/shard_map/all_to_all | solution.py:131
  24.2 1.8 copy.84
  26.0 2.3 reshape.126
  28.3 1.2 reshape.123
  29.4 1.1 copy.93
  30.6 0.0 all-to-all-done
  30.6 4.0 %all-to-all-start.2 = ((bf16[4,2,12288]{2,1,0:T(2,128)(2,1)}), bf16[4,2,12288]{2,1,0:T(2,128)(2,1)}, u32[]{:S(2)}, u32[]{:S(2)}) async-start(bf16[4,2,12288]{2,1,0:T(2,128)(2,1)} %reshape.126), calls=%async_computation.2 | async-start | bytes 393216 | tf_op jit(solution)/shard_map/all_to_all | solution.py:133
  34.6 0.0 reduce-scatter.2.cloned.1.call-start
  34.7 35.2 %all_gather.9 = bf16[8,4,16,768]{3,2,0,1:T(8,128)(2,1)S(1)} all-gather(bf16[8,1,16,768]{3,2,0,1:T(8,128)(2,1)S(1)} %bitcast.111), channel_id=1, replica_groups=mesh['clip'=2,'seq'=4,'head'=4] {'seq'}, dimensions={1}, use_global_device_ids=true | all-gather | bytes 983040 | tf_op jit(solution)/shard_map/all_gather | solution.py:151
  69.9 0.1 copy.82
  70.0 0.9 squeeze.9
  70.8 1.2 reshape.125
  72.0 1.1 copy.92
  73.1 0.2 reshape.115
  73.4 0.0 all-to-all-done.2
  73.4 5.6 %reshape.127 = bf16[3072,1,2,16]{3,2,1,0:T(2,128)(2,1)S(1)} reshape(bf16[4,2,12288]{2,1,0:T(2,128)(2,1)} %all-to-all-done.2) | data formatting | bytes 393216
  79.0 2.5 %copy.94 = bf16[2,1,16,4,768]{4,3,2,0,1:T(4,128)(2,1)} copy(bf16[2,1,16,4,768]{2,0,4,3,1:T(2,128)(2,1)S(1)} %bitcast.95) | data formatting | bytes 393216 | tf_op jit(solution)/shard_map/all_to_all | solution.py:133
  81.5 1.0 copy.86
  82.4 32.4 %all_gather.10 = bf16[8,4,16,768]{3,2,0,1:T(8,128)(2,1)S(1)} all-gather(bf16[8,1,16,768]{3,2,0,1:T(8,128)(2,1)S(1)} %bitcast.112), channel_id=1, replica_groups=mesh['clip'=2,'seq'=4,'head'=4] {'seq'}, dimensions={1}, use_global_device_ids=true | all-gather | bytes 983040 | tf_op jit(solution)/shard_map/all_gather | solution.py:152
  114.8 0.1 copy.87
  114.9 1.9 squeeze.10
  116.8 0.5 fusion.35
  117.3 0.5 fusion.8
  117.8 0.2 copy-done.2
  118.0 0.6 fusion.12
  118.7 0.1 copy.89
  118.8 0.2 dot_general.24
  119.1 0.0 copy-start.9
  119.1 0.0 copy-start.10
  119.1 57.9 %all-gather.2.cloned.1.call-done = bf16[768,5120]{1,0:T(8,128)(2,1)} async-done(((bf16[768,1280]{1,0:T(8,128)(2,1)}), bf16[768,5120]{1,0:T(8,128)(2,1)}) %all-gather.2.cloned.1.call-update) | async-done | bytes 7864336 | tf_op jit(solution)/shard_map/all_gather | solution.py:160
  177.0 5.6 %fusion.5 = bf16[8,1,16,5120]{3,2,0,1:T(8,128)(2,1)} fusion(bf16[8,16,768]{2,1,0:T(8,128)(2,1)S(1)} %dot_general.24, bf16[768,5120]{1,0:T(8,128)(2,1)} %all-gather.2.cloned.1.call-done), kind=kOutput, calls=%fused_computation.3 | convolution fusion | flops 1007288320 | bytes 9371648 | tf_op jit(solution)/shard_map/dot_general | solution.py:158
  182.6 0.0 reduce-scatter.2.cloned.1.call-update
  182.6 23.7 %reduce-scatter.2.cloned.1.call-done = bf16[2,1,16,5120]{3,2,0,1:T(8,128)(2,1)} async-done(((bf16[8,1,16,5120]{3,2,0,1:T(8,128)(2,1)}), bf16[2,1,16,5120]{3,2,0,1:T(8,128)(2,1)}) %reduce-scatter.2.cloned.1.call-update) | async-done | bytes 327696 | tf_op jit(solution)/shard_map/reduce_scatter | solution.py:164
  206.3 1.2 convert_reduce_fusion
  207.5 0.2 fusion.20
  207.7 0.0 copy-done.8
  207.8 0.2 fusion.23
  208.0 0.3 fusion.13
  208.3 0.1 reshape.117
  208.4 1.9 collective-permute-start
  210.4 3.3 %collective-permute-done = bf16[2,2,32,16]{3,2,1,0:T(8,128)(2,1)S(1)} collective-permute-done((bf16[2,2,32,16]{3,2,1,0:T(8,128)(2,1)S(1)}, bf16[2,2,32,16]{3,2,1,0:T(8,128)(2,1)S(1)}, u32[]{:S(2)}, u32[]{:S(2)}) %collective-permute-start) | collective-permute-done | bytes 4128 | tf_op jit(solution)/shard_map/ppermute | solution.py:12
  213.7 3.6 %collective-permute-start.1 = (bf16[4,1,32,16]{3,2,1,0:T(8,128)(2,1)S(1)}, bf16[4,1,32,16]{3,2,1,0:T(8,128)(2,1)S(1)}, u32[]{:S(2)}, u32[]{:S(2)}) collective-permute-start(bf16[4,1,32,16]{3,2,1,0:T(8,128)(2,1)S(1)} %get-tuple-element.63), channel_id=1, source_target_pairs={{0,4},{4,8},{8,12},{1,5},{5,9},{9,13},{2,6},{6,10},{10,14},{3,7},{... | collective-permute-start | bytes 12296 | tf_op jit(solution)/shard_map/ppermute | solution.py:22
  217.3 1.3 collective-permute-start.2
  218.6 0.3 collective-permute-done.1
  218.9 4.2 %collective-permute-done.2 = bf16[4,1,32,16]{3,2,1,0:T(8,128)(2,1)S(1)} collective-permute-done((bf16[4,1,32,16]{3,2,1,0:T(8,128)(2,1)S(1)}, bf16[4,1,32,16]{3,2,1,0:T(8,128)(2,1)S(1)}, u32[]{:S(2)}, u32[]{:S(2)}) %collective-permute-start.2) | collective-permute-done | bytes 4128 | tf_op jit(solution)/shard_map/ppermute | solution.py:23
  223.1 0.1 select_maximum_fusion
  223.2 0.0 copy-start.3
  223.2 0.0 copy-start.11
  223.2 0.0 copy-start.12
  223.2 0.1 fusion.32
  223.4 0.3 concatenate.105
  223.7 0.4 copy-done.3
  224.2 0.3 multiply_reduce_fusion
  224.5 0.8 multiply_convert_fusion
  (31 shorter events, 0.2 us)
Async XLA Ops:
  7.2 200.8 %copy-start = (bf16[5120,64]{0,1:T(8,128)(2,1)S(1)}, bf16[5120,64]{0,1:T(8,128)(2,1)}, u32[]{:S(2)}) copy-start(bf16[5120,64]{0,1:T(8,128)(2,1)} %param.21) | copy-start | bytes 1966084
  7.2 1.0 copy-start.5
  7.2 169.8 %all-gather.2.cloned.1.call-start = ((), (), s32[]{:S(2)}) async-start(), calls=%async_computation.4 | async-start | bytes 9830400 | tf_op jit(solution)/shard_map/all_gather | solution.py:160
  8.2 7.4 %copy-start.6 = (bf16[2,1,16,3072]{3,2,1,0:T(8,128)(2,1)S(1)}, bf16[2,1,16,3072]{3,2,1,0:T(8,128)(2,1)}, u32[]{:S(2)}) copy-start(bf16[2,1,16,3072]{3,2,1,0:T(8,128)(2,1)} %param.13) | copy-start | bytes 589828
  12.3 7.5 %all-to-all-start.1 = ((bf16[4,2,12288]{2,1,0:T(2,128)(2,1)}), bf16[4,2,12288]{2,1,0:T(2,128)(2,1)S(1)}, u32[]{:S(2)}, u32[]{:S(2)}) async-start(bf16[4,2,12288]{2,1,0:T(2,128)(2,1)} %reshape.122), calls=%async_computation.1 | async-start | bytes 393216 | tf_op jit(solution)/shard_map/all_to_all | solution.py:132
  17.5 6.7 %copy-start.7 = (bf16[2,1,16,3072]{3,2,1,0:T(8,128)(2,1)S(1)}, bf16[2,1,16,3072]{3,2,1,0:T(8,128)(2,1)}, u32[]{:S(2)}) copy-start(bf16[2,1,16,3072]{3,2,1,0:T(8,128)(2,1)} %param.15) | copy-start | bytes 589828
  19.8 10.8 %all-to-all-start = ((bf16[4,2,12288]{2,1,0:T(2,128)(2,1)}), bf16[4,2,12288]{2,1,0:T(2,128)(2,1)S(1)}, u32[]{:S(2)}, u32[]{:S(2)}) async-start(bf16[4,2,12288]{2,1,0:T(2,128)(2,1)} %reshape.124), calls=%async_computation | async-start | bytes 393216 | tf_op jit(solution)/shard_map/all_to_all | solution.py:131
  30.6 42.8 %all-to-all-start.2 = ((bf16[4,2,12288]{2,1,0:T(2,128)(2,1)}), bf16[4,2,12288]{2,1,0:T(2,128)(2,1)}, u32[]{:S(2)}, u32[]{:S(2)}) async-start(bf16[4,2,12288]{2,1,0:T(2,128)(2,1)} %reshape.126), calls=%async_computation.2 | async-start | bytes 393216 | tf_op jit(solution)/shard_map/all_to_all | solution.py:133
  34.6 171.7 %reduce-scatter.2.cloned.1.call-start = ((), (), s32[]{:S(2)}) async-start(), calls=%async_computation.5 | async-start | bytes 1638400 | tf_op jit(solution)/shard_map/reduce_scatter | solution.py:164
  116.8 1.2 copy-start.2
  119.1 63.5 %copy-start.9 = (f32[5120]{0:T(1024)S(1)}, f32[5120]{0:T(1024)}, u32[]{:S(2)}) copy-start(f32[5120]{0:T(1024)} %param.20) | copy-start | bytes 61444
  119.1 87.2 %copy-start.10 = (f32[5120]{0:T(1024)S(1)}, f32[5120]{0:T(1024)}, u32[]{:S(2)}) copy-start(f32[5120]{0:T(1024)} %param.18) | copy-start | bytes 61444
  182.6 23.8 %copy-start.4 = (bf16[2,1,16,5120]{3,2,1,0:T(8,128)(2,1)S(1)}, bf16[2,1,16,5120]{3,2,1,0:T(8,128)(2,1)}, u32[]{:S(2)}) copy-start(bf16[2,1,16,5120]{3,2,1,0:T(8,128)(2,1)} %param.16) | copy-start | bytes 983044
  182.6 25.2 %copy-start.8 = (f32[5120]{0:T(1024)S(1)}, f32[5120]{0:T(1024)}, u32[]{:S(2)}) copy-start(f32[5120]{0:T(1024)} %param.19) | copy-start | bytes 61444
  182.6 25.4 %copy-start.13 = (f32[64]{0:T(128)S(1)}, f32[64]{0:T(128)}, u32[]{:S(2)}) copy-start(f32[64]{0:T(128)} %param.22) | copy-start | bytes 772
  207.5 15.8 %copy-start.1 = (bf16[2,1,16,5120]{3,2,0,1:T(8,128)(2,1)}, bf16[2,1,16,5120]{3,2,0,1:T(8,128)(2,1)S(1)}, u32[]{:S(2)}) copy-start(bf16[2,1,16,5120]{3,2,0,1:T(8,128)(2,1)S(1)} %get-tuple-element.36) | copy-start | bytes 983044
  208.4 5.2 %collective-permute-start = (bf16[2,2,32,16]{3,2,1,0:T(8,128)(2,1)S(1)}, bf16[2,2,32,16]{3,2,1,0:T(8,128)(2,1)S(1)}, u32[]{:S(2)}, u32[]{:S(2)}) collective-permute-start(bf16[2,2,32,16]{3,2,1,0:T(8,128)(2,1)S(1)} %bitcast.101), channel_id=1, source_target_pairs={{0,1},{1,2},{2,3},{4,5},{5,6},{6,7},{8,9},{9,10},{10,11},{12,13},{... | collective-permute-start | bytes 12296 | tf_op jit(solution)/shard_map/ppermute | solution.py:12
  213.7 5.2 %collective-permute-start.1 = (bf16[4,1,32,16]{3,2,1,0:T(8,128)(2,1)S(1)}, bf16[4,1,32,16]{3,2,1,0:T(8,128)(2,1)S(1)}, u32[]{:S(2)}, u32[]{:S(2)}) collective-permute-start(bf16[4,1,32,16]{3,2,1,0:T(8,128)(2,1)S(1)} %get-tuple-element.63), channel_id=1, source_target_pairs={{0,4},{4,8},{8,12},{1,5},{5,9},{9,13},{2,6},{6,10},{10,14},{3,7},{... | collective-permute-start | bytes 12296 | tf_op jit(solution)/shard_map/ppermute | solution.py:22
  217.3 5.8 %collective-permute-start.2 = (bf16[4,1,32,16]{3,2,1,0:T(8,128)(2,1)S(1)}, bf16[4,1,32,16]{3,2,1,0:T(8,128)(2,1)S(1)}, u32[]{:S(2)}, u32[]{:S(2)}) collective-permute-start(bf16[4,1,32,16]{3,2,1,0:T(8,128)(2,1)S(1)} %get-tuple-element.64), channel_id=1, source_target_pairs={{4,0},{8,4},{12,8},{5,1},{9,5},{13,9},{6,2},{10,6},{14,10},{7,3},{... | collective-permute-start | bytes 12296 | tf_op jit(solution)/shard_map/ppermute | solution.py:23
  223.2 1.0 copy-start.3
  223.2 1.0 copy-start.11
  223.2 1.3 copy-start.12
Sparse Core Ops, SparseCore 0:
  9.6 167.3 all-gather.1
  182.7 23.5 reduce-scatter.1
where the time goes:
time: 233 us; the launch traced here: 232 us
  waiting for transfers between devices  90.1 us (39%)
  blocking collectives  67.6 us (29%)
  local copies, waits for them, and re-layouts  30.9 us (13%)
  starting transfers between devices  18.7 us (8%)
  between operations  14.4 us (6%)
  matrix products  7.28 us (3%)
  other arithmetic  3.08 us (1%)
    all_gather x1, waiting for transfers between devices, on_device(): lax.all_gather(out_weight, 'seq', axis=1, tiled=True)  57.9 us
    all_gather x1, blocking collectives, on_device(): lax.all_gather(local_keys, 'seq', axis=1, tiled=True)  35.2 us
    all_gather x1, blocking collectives, on_device(): lax.all_gather(local_values, 'seq', axis=1, tiled=True)  32.4 us
    reduce_scatter x1, waiting for transfers between devices, on_device(): lax.psum_scatter(partial_value.astype(jnp.bfloat16), 'head', scatter_dime...  23.7 us
    unnamed x37, local copies, waits for them, and re-layouts  21.1 us
    dot_general x1, matrix products, on_device(): jnp.dot(attended, lax.all_gather(out_weight, 'seq', axis=1, tiled=True),...  5.58 us
  transfers between devices with their start and end apart: 8, of which 5 were waited for; matrix products, arithmetic and copies ran while one was open for 13% of the time, Pallas kernels for 0%

commit v1 on v0

--- a/solution.py
+++ b/solution.py
@@ -157,7 +157,7 @@
     attended = attended.transpose(1, 0, 2).reshape(count, group_width)
     partial_value = jnp.dot(
         attended,
-        lax.all_gather(out_weight, "seq", axis=1, tiled=True),
+        jnp.concatenate(lax.all_gather(out_weight, "seq"), axis=1),
         preferred_element_type=jnp.float32,
     )
     partial_value = partial_value.reshape(frames_all, height, breadth, partial_value.shape[-1])

time: 233 us -> 259 us (1.11)
  local copies, waits for them, and re-layouts: 30.9 us -> 57.3 us
    reshape x0 -> x1, local copies, waits for them, and re-layouts: none -> 13.9 us  [on_device(): jnp.concatenate(lax.all_gather(out_weight, 'seq'), axis=1)]
    all_gather x0 -> x1, local copies, waits for them, and re-layouts: none -> 12.4 us  [on_device(): lax.all_gather(out_weight, 'seq')]
  transfers between devices with their start and end apart: 8 -> 8, of which waited for: 5 -> 5; matrix products, arithmetic and copies ran while one was open for 13% -> 12% of each run, Pallas kernels for 0% -> 0%
where the time goes in v1:
time: 259 us; the launch traced here: 258 us
  waiting for transfers between devices  90.1 us (35%)
  blocking collectives  67.6 us (26%)
  local copies, waits for them, and re-layouts  57.3 us (22%)
  starting transfers between devices  18.7 us (7%)
  between operations  14.4 us (6%)
  matrix products  7.29 us (3%)
  other arithmetic  3.07 us (1%)
    all_gather x1, waiting for transfers between devices, on_device(): lax.all_gather(out_weight, 'seq')  58 us
    all_gather x1, blocking collectives, on_device(): lax.all_gather(local_keys, 'seq', axis=1, tiled=True)  35.2 us
    all_gather x1, blocking collectives, on_device(): lax.all_gather(local_values, 'seq', axis=1, tiled=True)  32.3 us
    reduce_scatter x1, waiting for transfers between devices, on_device(): lax.psum_scatter(partial_value.astype(jnp.bfloat16), 'head', scatter_dime...  23.7 us
    unnamed x37, local copies, waits for them, and re-layouts  21.1 us
    reshape x1, local copies, waits for them, and re-layouts, on_device(): jnp.concatenate(lax.all_gather(out_weight, 'seq'), axis=1)  13.9 us
    all_gather x1, local copies, waits for them, and re-layouts, on_device(): lax.all_gather(out_weight, 'seq')  12.4 us
    dot_general x1, matrix products, on_device(): jnp.dot(attended, jnp.concatenate(lax.all_gather(out_weight, 'seq'), axis...  5.59 us
  transfers between devices with their start and end apart: 8, of which 5 were waited for; matrix products, arithmetic and copies ran while one was open for 12% of the time, Pallas kernels for 0%

profile of v1, /device:TPU:2, one launch (start us, length us, event | category | flops | bytes accessed | tf_op | source)
XLA Modules:
  0.0 258.5 jit_solution(16982671155406756970)
XLA Ops:
  7.2 0.0 copy-start
  7.2 0.0 all-gather.3.cloned.1.call-start
  7.2 0.7 all-gather.3.cloned.1.call-update
  7.9 0.2 copy-done.5
  8.2 1.8 copy.84
  10.0 2.3 reshape.132
  12.3 3.4 %all-to-all-start.1 = ((bf16[4,2,12288]{2,1,0:T(2,128)(2,1)}), bf16[4,2,12288]{2,1,0:T(2,128)(2,1)S(1)}, u32[]{:S(2)}, u32[]{:S(2)}) async-start(bf16[4,2,12288]{2,1,0:T(2,128)(2,1)} %reshape.132), calls=%async_computation.1 | async-start | bytes 393216 | tf_op jit(solution)/shard_map/all_to_all | solution.py:132
  15.6 0.0 copy-start.7
  15.6 1.8 copy.80
  17.5 2.3 reshape.134
  19.8 4.4 %all-to-all-start = ((bf16[4,2,12288]{2,1,0:T(2,128)(2,1)}), bf16[4,2,12288]{2,1,0:T(2,128)(2,1)S(1)}, u32[]{:S(2)}, u32[]{:S(2)}) async-start(bf16[4,2,12288]{2,1,0:T(2,128)(2,1)} %reshape.134), calls=%async_computation | async-start | bytes 393216 | tf_op jit(solution)/shard_map/all_to_all | solution.py:131
  24.2 1.8 copy.89
  26.0 2.3 reshape.136
  28.3 1.2 reshape.133
  29.4 1.1 copy.99
  30.6 0.0 all-to-all-done
  30.6 4.0 %all-to-all-start.2 = ((bf16[4,2,12288]{2,1,0:T(2,128)(2,1)}), bf16[4,2,12288]{2,1,0:T(2,128)(2,1)}, u32[]{:S(2)}, u32[]{:S(2)}) async-start(bf16[4,2,12288]{2,1,0:T(2,128)(2,1)} %reshape.136), calls=%async_computation.2 | async-start | bytes 393216 | tf_op jit(solution)/shard_map/all_to_all | solution.py:133
  34.6 0.0 reduce-scatter.2.cloned.1.call-start
  34.7 35.2 %all_gather.12 = bf16[8,4,16,768]{3,2,0,1:T(8,128)(2,1)S(1)} all-gather(bf16[8,1,16,768]{3,2,0,1:T(8,128)(2,1)S(1)} %bitcast.111), channel_id=1, replica_groups=mesh['clip'=2,'seq'=4,'head'=4] {'seq'}, dimensions={1}, use_global_device_ids=true | all-gather | bytes 983040 | tf_op jit(solution)/shard_map/all_gather | solution.py:151
  69.9 1.2 reshape.135
  71.1 1.1 copy.98
  72.2 0.2 reshape.121
  72.4 0.1 copy.87
  72.5 0.9 squeeze.9
  73.4 0.0 all-to-all-done.2
  73.4 5.6 %reshape.137 = bf16[3072,1,2,16]{3,2,1,0:T(2,128)(2,1)S(1)} reshape(bf16[4,2,12288]{2,1,0:T(2,128)(2,1)} %all-to-all-done.2) | data formatting | bytes 393216
  79.0 2.5 copy.100
  81.5 1.0 copy.91
  82.4 32.3 %all_gather.13 = bf16[8,4,16,768]{3,2,0,1:T(8,128)(2,1)S(1)} all-gather(bf16[8,1,16,768]{3,2,0,1:T(8,128)(2,1)S(1)} %bitcast.112), channel_id=1, replica_groups=mesh['clip'=2,'seq'=4,'head'=4] {'seq'}, dimensions={1}, use_global_device_ids=true | all-gather | bytes 983040 | tf_op jit(solution)/shard_map/all_gather | solution.py:152
  114.8 0.1 copy.92
  114.9 1.9 squeeze.10
  116.8 0.5 fusion.28
  117.2 0.5 fusion.1
  117.8 0.2 copy-done.2
  118.0 0.6 fusion.5
  118.6 0.1 copy.94
  118.8 0.2 dot_general.24
  119.0 58.0 %all-gather.3.cloned.1.call-done = bf16[3072,1280]{1,0:T(8,128)(2,1)} async-done(((bf16[768,1280]{1,0:T(8,128)(2,1)}), bf16[3072,1280]{1,0:T(8,128)(2,1)}) %all-gather.3.cloned.1.call-update) | async-done | bytes 7864336 | tf_op jit(solution)/shard_map/all_gather | solution.py:160
  177.0 12.4 %copy.114 = bf16[4,768,1280]{2,0,1:T(4,128)(2,1)} copy(bf16[4,768,1280]{2,1,0:T(8,128)(2,1)} %bitcast.92) | data formatting | bytes 15728640 | tf_op jit(solution)/shard_map/all_gather | solution.py:160
  189.4 13.9 %reshape.130 = bf16[768,5120,1]{1,0,2:T(8,128)(2,1)} reshape(bf16[768,4,1280]{2,1,0:T(4,128)(2,1)} %bitcast.91) | data formatting | bytes 15728640 | tf_op jit(solution)/shard_map/reshape | solution.py:160
  203.4 5.6 %fusion = bf16[8,1,16,5120]{3,2,0,1:T(8,128)(2,1)} fusion(bf16[8,16,768]{2,1,0:T(8,128)(2,1)S(1)} %dot_general.24, bf16[768,5120,1]{1,0,2:T(8,128)(2,1)} %reshape.130), kind=kOutput, calls=%fused_computation.2 | convolution fusion | flops 1007288320 | bytes 9371648 | tf_op jit(solution)/shard_map/dot_general | solution.py:158
  209.0 0.0 reduce-scatter.2.cloned.1.call-update
  209.0 23.7 %reduce-scatter.2.cloned.1.call-done = bf16[2,1,16,5120]{3,2,0,1:T(8,128)(2,1)} async-done(((bf16[8,1,16,5120]{3,2,0,1:T(8,128)(2,1)}), bf16[2,1,16,5120]{3,2,0,1:T(8,128)(2,1)}) %reduce-scatter.2.cloned.1.call-update) | async-done | bytes 327696 | tf_op jit(solution)/shard_map/reduce_scatter | solution.py:164
  232.7 1.2 convert_reduce_fusion
  233.9 0.2 fusion.13
  234.1 0.0 copy-done.8
  234.1 0.2 fusion.16
  234.4 0.3 fusion.6
  234.7 0.1 reshape.125
  234.8 1.9 collective-permute-start
  236.7 3.3 %collective-permute-done = bf16[2,2,32,16]{3,2,1,0:T(8,128)(2,1)S(1)} collective-permute-done((bf16[2,2,32,16]{3,2,1,0:T(8,128)(2,1)S(1)}, bf16[2,2,32,16]{3,2,1,0:T(8,128)(2,1)S(1)}, u32[]{:S(2)}, u32[]{:S(2)}) %collective-permute-start) | collective-permute-done | bytes 4128 | tf_op jit(solution)/shard_map/ppermute | solution.py:12
  240.0 3.6 %collective-permute-start.1 = (bf16[4,1,32,16]{3,2,1,0:T(8,128)(2,1)S(1)}, bf16[4,1,32,16]{3,2,1,0:T(8,128)(2,1)S(1)}, u32[]{:S(2)}, u32[]{:S(2)}) collective-permute-start(bf16[4,1,32,16]{3,2,1,0:T(8,128)(2,1)S(1)} %get-tuple-element.63), channel_id=1, source_target_pairs={{0,4},{4,8},{8,12},{1,5},{5,9},{9,13},{2,6},{6,10},{10,14},{3,7},{... | collective-permute-start | bytes 12296 | tf_op jit(solution)/shard_map/ppermute | solution.py:22
  243.7 1.3 collective-permute-start.2
  245.0 0.3 collective-permute-done.1
  245.3 4.2 %collective-permute-done.2 = bf16[4,1,32,16]{3,2,1,0:T(8,128)(2,1)S(1)} collective-permute-done((bf16[4,1,32,16]{3,2,1,0:T(8,128)(2,1)S(1)}, bf16[4,1,32,16]{3,2,1,0:T(8,128)(2,1)S(1)}, u32[]{:S(2)}, u32[]{:S(2)}) %collective-permute-start.2) | collective-permute-done | bytes 4128 | tf_op jit(solution)/shard_map/ppermute | solution.py:23
  249.5 0.1 select_maximum_fusion
  249.6 0.0 copy-start.3
  249.6 0.0 copy-start.11
  249.6 0.0 copy-start.12
  249.6 0.1 fusion.25
  249.8 0.3 concatenate.105
  250.1 0.4 copy-done.3
  250.5 0.3 multiply_reduce_fusion
  250.9 0.8 multiply_convert_fusion
  (33 shorter events, 0.2 us)
Async XLA Ops:
  7.2 227.2 %copy-start = (bf16[5120,64]{0,1:T(8,128)(2,1)S(1)}, bf16[5120,64]{0,1:T(8,128)(2,1)}, u32[]{:S(2)}) copy-start(bf16[5120,64]{0,1:T(8,128)(2,1)} %param.21) | copy-start | bytes 1966084
  7.2 1.0 copy-start.5
  7.2 169.8 %all-gather.3.cloned.1.call-start = ((), (), s32[]{:S(2)}) async-start(), calls=%async_computation.5 | async-start | bytes 9830400 | tf_op jit(solution)/shard_map/all_gather | solution.py:160
  8.2 7.4 %copy-start.6 = (bf16[2,1,16,3072]{3,2,1,0:T(8,128)(2,1)S(1)}, bf16[2,1,16,3072]{3,2,1,0:T(8,128)(2,1)}, u32[]{:S(2)}) copy-start(bf16[2,1,16,3072]{3,2,1,0:T(8,128)(2,1)} %param.13) | copy-start | bytes 589828
  12.3 7.5 %all-to-all-start.1 = ((bf16[4,2,12288]{2,1,0:T(2,128)(2,1)}), bf16[4,2,12288]{2,1,0:T(2,128)(2,1)S(1)}, u32[]{:S(2)}, u32[]{:S(2)}) async-start(bf16[4,2,12288]{2,1,0:T(2,128)(2,1)} %reshape.132), calls=%async_computation.1 | async-start | bytes 393216 | tf_op jit(solution)/shard_map/all_to_all | solution.py:132
  15.6 8.6 %copy-start.7 = (bf16[2,1,16,3072]{3,2,1,0:T(8,128)(2,1)S(1)}, bf16[2,1,16,3072]{3,2,1,0:T(8,128)(2,1)}, u32[]{:S(2)}) copy-start(bf16[2,1,16,3072]{3,2,1,0:T(8,128)(2,1)} %param.15) | copy-start | bytes 589828
  19.8 10.8 %all-to-all-start = ((bf16[4,2,12288]{2,1,0:T(2,128)(2,1)}), bf16[4,2,12288]{2,1,0:T(2,128)(2,1)S(1)}, u32[]{:S(2)}, u32[]{:S(2)}) async-start(bf16[4,2,12288]{2,1,0:T(2,128)(2,1)} %reshape.134), calls=%async_computation | async-start | bytes 393216 | tf_op jit(solution)/shard_map/all_to_all | solution.py:131
  30.6 42.8 %all-to-all-start.2 = ((bf16[4,2,12288]{2,1,0:T(2,128)(2,1)}), bf16[4,2,12288]{2,1,0:T(2,128)(2,1)}, u32[]{:S(2)}, u32[]{:S(2)}) async-start(bf16[4,2,12288]{2,1,0:T(2,128)(2,1)} %reshape.136), calls=%async_computation.2 | async-start | bytes 393216 | tf_op jit(solution)/shard_map/all_to_all | solution.py:133
  34.6 198.1 %reduce-scatter.2.cloned.1.call-start = ((), (), s32[]{:S(2)}) async-start(), calls=%async_computation.4 | async-start | bytes 1638400 | tf_op jit(solution)/shard_map/reduce_scatter | solution.py:164
  116.8 1.2 copy-start.2
  203.4 5.6 %copy-start.9 = (f32[5120]{0:T(1024)S(1)}, f32[5120]{0:T(1024)}, u32[]{:S(2)}) copy-start(f32[5120]{0:T(1024)} %param.20) | copy-start | bytes 61444
  203.4 29.3 %copy-start.10 = (f32[5120]{0:T(1024)S(1)}, f32[5120]{0:T(1024)}, u32[]{:S(2)}) copy-start(f32[5120]{0:T(1024)} %param.18) | copy-start | bytes 61444
  209.0 23.7 %copy-start.4 = (bf16[2,1,16,5120]{3,2,1,0:T(8,128)(2,1)S(1)}, bf16[2,1,16,5120]{3,2,1,0:T(8,128)(2,1)}, u32[]{:S(2)}) copy-start(bf16[2,1,16,5120]{3,2,1,0:T(8,128)(2,1)} %param.16) | copy-start | bytes 983044
  209.0 25.2 %copy-start.8 = (f32[5120]{0:T(1024)S(1)}, f32[5120]{0:T(1024)}, u32[]{:S(2)}) copy-start(f32[5120]{0:T(1024)} %param.19) | copy-start | bytes 61444
  209.0 25.4 %copy-start.13 = (f32[64]{0:T(128)S(1)}, f32[64]{0:T(128)}, u32[]{:S(2)}) copy-start(f32[64]{0:T(128)} %param.22) | copy-start | bytes 772
  233.9 15.8 %copy-start.1 = (bf16[2,1,16,5120]{3,2,0,1:T(8,128)(2,1)}, bf16[2,1,16,5120]{3,2,0,1:T(8,128)(2,1)S(1)}, u32[]{:S(2)}) copy-start(bf16[2,1,16,5120]{3,2,0,1:T(8,128)(2,1)S(1)} %get-tuple-element.36) | copy-start | bytes 983044
  234.8 5.2 %collective-permute-start = (bf16[2,2,32,16]{3,2,1,0:T(8,128)(2,1)S(1)}, bf16[2,2,32,16]{3,2,1,0:T(8,128)(2,1)S(1)}, u32[]{:S(2)}, u32[]{:S(2)}) collective-permute-start(bf16[2,2,32,16]{3,2,1,0:T(8,128)(2,1)S(1)} %bitcast.101), channel_id=1, source_target_pairs={{0,1},{1,2},{2,3},{4,5},{5,6},{6,7},{8,9},{9,10},{10,11},{12,13},{... | collective-permute-start | bytes 12296 | tf_op jit(solution)/shard_map/ppermute | solution.py:12
  240.0 5.2 %collective-permute-start.1 = (bf16[4,1,32,16]{3,2,1,0:T(8,128)(2,1)S(1)}, bf16[4,1,32,16]{3,2,1,0:T(8,128)(2,1)S(1)}, u32[]{:S(2)}, u32[]{:S(2)}) collective-permute-start(bf16[4,1,32,16]{3,2,1,0:T(8,128)(2,1)S(1)} %get-tuple-element.63), channel_id=1, source_target_pairs={{0,4},{4,8},{8,12},{1,5},{5,9},{9,13},{2,6},{6,10},{10,14},{3,7},{... | collective-permute-start | bytes 12296 | tf_op jit(solution)/shard_map/ppermute | solution.py:22
  243.7 5.8 %collective-permute-start.2 = (bf16[4,1,32,16]{3,2,1,0:T(8,128)(2,1)S(1)}, bf16[4,1,32,16]{3,2,1,0:T(8,128)(2,1)S(1)}, u32[]{:S(2)}, u32[]{:S(2)}) collective-permute-start(bf16[4,1,32,16]{3,2,1,0:T(8,128)(2,1)S(1)} %get-tuple-element.64), channel_id=1, source_target_pairs={{4,0},{8,4},{12,8},{5,1},{9,5},{13,9},{6,2},{10,6},{14,10},{7,3},{... | collective-permute-start | bytes 12296 | tf_op jit(solution)/shard_map/ppermute | solution.py:23
  249.6 1.0 copy-start.3
  249.6 1.0 copy-start.11
  249.6 1.3 copy-start.12
Sparse Core Ops, SparseCore 0:
  9.6 167.3 all-gather.2
  209.1 23.5 reduce-scatter.1
